TPU v7x, 32 devices: a whole 2x2x4 slice. The times are simulated.
32 devices in a mesh: dp: 16 (over z, x, core), mp: 2 (over y).
Axes of the slice: x: 2, y: 2, z: 4, core: 2. Of those that a mesh axis runs over, the one named last changes fastest.
Arguments:
- context: bfloat16 [5120, 2048], P('dp', 'mp'), may hold values from -6 to 6
- out_weight: bfloat16 [2048, 3584], P('mp'), may hold values from -0.125 to 0.125
- cotangent: bfloat16 [5120, 3584], P('dp'), may hold values from -0.059814453 to 0.059814453
- norm_gain: float32 [3584], replicated, may hold values from 0.5 to 1.5
- first_moment: float32 [2, 1024, 3584], P('mp', 'dp'), may hold values from -6 to 6
- second_moment: float32 [2, 1024, 3584], P('mp', 'dp'), may hold values from 0.01 to 1
Outputs:
- new_weight: bfloat16 [2, 1024, 3584], P('mp', 'dp')
- new_first: float32 [2, 1024, 3584], P('mp', 'dp')
- new_second: float32 [2, 1024, 3584], P('mp', 'dp')
- grad_gain: float32 [3584], replicated
- grad_context: bfloat16 [5120, 2048], P('dp', 'mp')
All inputs are finite; a program needn't handle non-finite values.
Results may differ from a plain program's by a relative error of at most 0.005.
Values may be sent and summed in bfloat16 or wider, within the bound.
A program may use at most 128 MiB of HBM per device.

v0:
```python
import jax
import jax.numpy as jnp
from jax import lax
from jax.sharding import PartitionSpec as P

norm_floor = 0.1
learn_rate = 0.01
beta_one = 0.9
beta_two = 0.95
adam_floor = 1e-08


def adam_update(master, first_moment, second_moment, grad_shard):
    new_first = beta_one * first_moment + (1.0 - beta_one) * grad_shard
    new_second = beta_two * second_moment + (1.0 - beta_two) * grad_shard * grad_shard
    new_weight = (master - learn_rate * new_first / (jnp.sqrt(new_second) + adam_floor)).astype(
        jnp.bfloat16
    )
    return (new_weight, new_first, new_second)


def per_device(context, out_weight, cotangent, norm_gain, first_moment, second_moment):
    width = out_weight.shape[1]
    partial_value = jnp.dot(context, out_weight, preferred_element_type=jnp.float32)
    half_width = width // lax.axis_size("mp")
    offset = lax.axis_index("mp") * half_width
    attn_half = lax.psum_scatter(partial_value, "mp", scatter_dimension=1, tiled=True)
    gain_half = lax.dynamic_slice_in_dim(norm_gain, offset, half_width, 0)
    upstream = lax.dynamic_slice_in_dim(cotangent, offset, half_width, 1).astype(jnp.float32)
    squares = jnp.sum(attn_half * attn_half, axis=-1, keepdims=True)
    total_sq = lax.psum(squares, "mp")
    inverse = lax.rsqrt(total_sq / width + norm_floor)
    normed = attn_half * inverse
    scaled = upstream * gain_half
    product_half = jnp.sum(scaled * normed, axis=-1, keepdims=True)
    product_all = lax.psum(product_half, "mp")
    grad_half = (inverse * (scaled - normed * (product_all / width))).astype(jnp.bfloat16)
    grad_attn = lax.all_gather(grad_half, "mp", axis=1, tiled=True)
    gain_part = jnp.sum(upstream * normed, axis=0)
    gain_total = lax.psum(gain_part, "dp")
    grad_gain = lax.all_gather(gain_total, "mp", axis=0, tiled=True)
    shard_rows = first_moment.shape[1]
    master = lax.dynamic_slice_in_dim(
        out_weight, lax.axis_index("dp") * shard_rows, shard_rows, 0
    ).astype(jnp.float32)[None]
    grad_shard = lax.psum_scatter(
        lax.dot_general(
            context, grad_attn, (((0,), (0,)), ((), ())), preferred_element_type=jnp.float32
        ),
        "dp",
        scatter_dimension=0,
        tiled=True,
    )
    grad_context = lax.dot_general(
        grad_attn, out_weight, (((1,), (1,)), ((), ())), preferred_element_type=jnp.float32
    ).astype(jnp.bfloat16)
    new_weight, new_first, new_second = adam_update(
        master, first_moment, second_moment, grad_shard[None]
    )
    return (new_weight, new_first, new_second, grad_gain, grad_context)


def solution(mesh):
    return jax.shard_map(
        per_device,
        mesh=mesh,
        in_specs=(
            P("dp", "mp"),
            P("mp", None),
            P("dp", None),
            P(),
            P("mp", "dp", None),
            P("mp", "dp", None),
        ),
        out_specs=(
            P("mp", "dp", None),
            P("mp", "dp", None),
            P("mp", "dp", None),
            P(),
            P("dp", "mp"),
        ),
        check_vma=False,
    )
```

profile of v0, /device:TPU:0, one launch (start us, length us, event | category | flops | bytes accessed | tf_op | source)
XLA Modules:
  0.0 323.5 jit_solution(9615545915211681465)
XLA Ops:
  7.2 1.0 copy-done
  8.3 7.7 %fusion.10 = f32[320,3584]{1,0:T(8,128)} fusion(bf16[320,1024]{1,0:T(8,128)(2,1)S(1)} %copy-done, bf16[1024,3584]{1,0:T(8,128)(2,1)} %param.7), kind=kOutput, calls=%fused_computation.20 | convolution fusion | flops 2348810240 | bytes 12582912 | tf_op jit(solution)/shard_map/dot_general | solution.py:24
  16.0 0.6 copy-done.5
  16.7 60.8 %reduce-scatter.5.cloned.1.call-done = f32[320,1792]{1,0:T(8,128)} async-done(((f32[320,3584]{1,0:T(8,128)}), f32[320,1792]{1,0:T(8,128)}) %reduce-scatter.5.cloned.1.call-update) | async-done | bytes 2293776 | tf_op jit(solution)/shard_map/reduce_scatter | solution.py:27
  77.5 2.0 multiply_reduce_fusion
  79.5 4.9 %psum.21 = f32[320,1]{0,1:T(1,128)S(1)} all-reduce(f32[320,1]{0,1:T(1,128)S(1)} %broadcast_in_dim.16), channel_id=1, replica_groups=mesh['dp'=16,'mp'=2] {'mp'}, use_global_device_ids=true, to_apply=%region_2.0 | all-reduce | flops 320 | bytes 2560 | tf_op jit(solution)/shard_map/psum | solution.py:31
  84.5 2.1 fusion.5
  86.6 4.9 %psum.22 = f32[320,1]{0,1:T(1,128)S(1)} all-reduce(f32[320,1]{0,1:T(1,128)S(1)} %broadcast_in_dim.17), channel_id=1, replica_groups=mesh['dp'=16,'mp'=2] {'mp'}, use_global_device_ids=true, to_apply=%region_4.0 | all-reduce | flops 320 | bytes 2560 | tf_op jit(solution)/shard_map/psum | solution.py:36
  91.5 2.8 fusion.4
  94.4 35.4 %all-gather.3.cloned.1.call-done = bf16[320,3584]{1,0:T(8,128)(2,1)} async-done(((bf16[320,1792]{1,0:T(8,128)(2,1)}), bf16[320,3584]{1,0:T(8,128)(2,1)}) %all-gather.3.cloned.1.call-update) | async-done | bytes 2293776 | tf_op jit(solution)/shard_map/all_gather | solution.py:38
  129.8 8.9 %convolution_bitcast_fusion = f32[1024,3584]{0,1:T(8,128)} fusion(bf16[320,3584]{1,0:T(8,128)(2,1)} %all-gather.3.cloned.1.call-done, bf16[320,1024]{1,0:T(8,128)(2,1)S(1)} %copy-done), kind=kOutput, calls=%fused_computation | convolution fusion | flops 2348810240 | bytes 17629184 | tf_op jit(solution)/shard_map/dot_general | solution.py:47
  138.8 14.3 %copy.29 = f32[1024,3584]{1,0:T(8,128)} copy(f32[1024,3584]{0,1:T(8,128)} %convolution_bitcast_fusion) | data formatting | bytes 29360128
  153.1 1.1 constant_dynamic-slice_fusion
  154.6 1.7 copy.24
  156.4 3.0 copy.25
  159.3 33.6 %psum.23 = f32[1792]{0:T(1024)S(1)} all-reduce(f32[1792]{0:T(1024)S(1)} %get-tuple-element.20), channel_id=1, replica_groups=mesh['dp'=16,'mp'=2] {'dp'}, use_global_device_ids=true, to_apply=%region_7.0 | all-reduce | flops 1792 | bytes 14336 | tf_op jit(solution)/shard_map/psum | solution.py:40
  192.9 4.4 %all-gather = f32[2,1,1792]{2,1,0:T(1,128)S(1)} all-gather(f32[1,1,1792]{2,1,0:T(1,128)S(1)} %reshape.15), channel_id=1, replica_groups=mesh['dp'=16,'mp'=2] {'mp'}, dimensions={0}, use_global_device_ids=true | all-gather | bytes 21504 | tf_op jit(solution)/shard_map/all_gather | solution.py:41
  198.0 7.3 %convolution_convert_fusion = bf16[320,1024]{1,0:T(8,128)(2,1)} fusion(bf16[320,3584]{1,0:T(8,128)(2,1)} %all-gather.3.cloned.1.call-done, bf16[1024,3584]{1,0:T(8,128)(2,1)} %param.7), kind=kOutput, calls=%fused_computation.16 | convolution fusion | flops 2349137920 | bytes 10289152 | tf_op jit(solution)/shard_map/dot_general | solution.py:54
  205.3 98.2 %reduce-scatter.7.cloned.1.call-done = f32[64,3584]{1,0:T(8,128)} async-done(((f32[1024,3584]{1,0:T(8,128)}), f32[64,3584]{1,0:T(8,128)}) %reduce-scatter.7.cloned.1.call-update) | async-done | bytes 917520
  303.4 3.0 copy.30
  306.4 4.9 %fusion.8 = (bf16[1,64,3584]{1,2,0:T(8,128)(2,1)}, f32[1,64,3584]{1,2,0:T(8,128)}, f32[1,64,3584]{1,2,0:T(8,128)}) fusion(bf16[64,3584]{0,1:T(8,128)(2,1)S(1)} %copy.31, f32[64,3584]{0,1:T(8,128)} %copy.30, f32[1,64,3584]{1,2,0:T(8,128)S(1)} %copy.24, f32[1,64,3584]{1,2,0:T(8,128)} %copy.25), kind=kLoop, calls=%fused_computation.14 | loop fusion | flops 2981888 | bytes 5505024 | tf_op jit(solution)/shard_map/convert_element_type | solution.py:16
  311.3 3.1 copy.27
  314.4 1.4 copy.28
  315.9 1.1 copy.26
  (25 shorter events, 1.4 us)
Async XLA Ops:
  7.2 1.1 copy-start
  7.2 70.3 %reduce-scatter.5.cloned.1.call-start = ((), (), s32[]{:S(2)}) async-start(), calls=%async_computation.2 | async-start | bytes 6881280 | tf_op jit(solution)/shard_map/reduce_scatter | solution.py:27
  15.9 0.7 copy-start.5
  16.0 113.9 %all-gather.3.cloned.1.call-start = ((), (), s32[]{:S(2)}) async-start(), calls=%async_computation.3 | async-start | bytes 3440640 | tf_op jit(solution)/shard_map/all_gather | solution.py:38
  77.5 7.0 %copy-start.2 = (f32[320,1792]{1,0:T(8,128)S(1)}, f32[320,1792]{1,0:T(8,128)}, u32[]{:S(2)}) copy-start(f32[320,1792]{1,0:T(8,128)} %reduce-scatter.5.cloned.1.call-done) | copy-start | bytes 6881284
  94.4 209.1 %reduce-scatter.7.cloned.1.call-start = ((), (), s32[]{:S(2)}) async-start(), calls=%async_computation.4 | async-start | bytes 15597568
  311.3 3.1 copy-start.3
  311.3 4.5 %copy-start.4 = (bf16[1,64,3584]{1,2,0:T(8,128)(2,1)S(1)}, bf16[1,64,3584]{1,2,0:T(8,128)(2,1)}, u32[]{:S(2)}) copy-start(bf16[1,64,3584]{1,2,0:T(8,128)(2,1)} %get-tuple-element.22) | copy-start | bytes 1376260
  311.3 5.6 %copy-start.1 = (bf16[320,1024]{1,0:T(8,128)(2,1)S(1)}, bf16[320,1024]{1,0:T(8,128)(2,1)}, u32[]{:S(2)}) copy-start(bf16[320,1024]{1,0:T(8,128)(2,1)} %param.6) | copy-start | bytes 1966084
Sparse Core Ops, SparseCore 0:
  16.1 61.3 reduce-scatter.4
  94.5 35.3 all-gather.2
  153.3 150.1 reduce-scatter.6
where the time goes:
time: 324 us; the launch traced here: 323 us
  waiting for transfers between devices  194 us (60%)
  blocking collectives  47.8 us (15%)
  local copies, waits for them, and re-layouts  31.5 us (10%)
  matrix products  23.9 us (7%)
  between operations  13.8 us (4%)
  other arithmetic  11.9 us (4%)
    unnamed x4, waiting for transfers between devices  98.2 us
    reduce_scatter x1, waiting for transfers between devices, per_device(): lax.psum_scatter(partial_value, 'mp', scatter_dimension=1, tiled=True)  60.8 us
    all_gather x1, waiting for transfers between devices, per_device(): grad_attn = lax.all_gather(grad_half, 'mp', axis=1, tiled=True)  35.4 us
    psum x1, blocking collectives, per_device(): gain_total = lax.psum(gain_part, 'dp')  33.6 us
    unnamed x22, local copies, waits for them, and re-layouts  30.3 us
    dot_general x1, matrix products, per_device(): lax.dot_general(context, grad_attn, (((0,), (0,)), ((), ())), preferred_e...  8.95 us
    dot_general x1, matrix products, per_device(): jnp.dot(context, out_weight, preferred_element_type=jnp.float32)  7.67 us
    dot_general x1, matrix products, per_device(): lax.dot_general(grad_attn, out_weight, (((1,), (1,)), ((), ())), preferre...  7.26 us
  transfers between devices with their start and end apart: 3, of which 3 were waited for; matrix products, arithmetic and copies ran while one was open for 4% of the time, Pallas kernels for 0%

commit v1 on v0

--- a/solution.py
+++ b/solution.py
@@ -37,7 +37,7 @@
     grad_half = (inverse * (scaled - normed * (product_all / width))).astype(jnp.bfloat16)
     grad_attn = lax.all_gather(grad_half, "mp", axis=1, tiled=True)
     gain_part = jnp.sum(upstream * normed, axis=0)
-    gain_total = lax.psum(gain_part, "dp")
+    gain_total = jnp.sum(lax.all_gather(gain_part, "dp"), axis=0)
     grad_gain = lax.all_gather(gain_total, "mp", axis=0, tiled=True)
     shard_rows = first_moment.shape[1]
     master = lax.dynamic_slice_in_dim(

time: 324 us -> 324 us (level)
  waiting for transfers between devices: 194 us -> 206 us
  blocking collectives: 47.8 us -> 35.9 us
    psum x1 -> x0, blocking collectives: 33.6 us -> none  [per_device(): gain_total = lax.psum(gain_part, 'dp')]
    all_gather x0 -> x1, blocking collectives: none -> 21.6 us  [per_device(): gain_total = jnp.sum(lax.all_gather(gain_part, 'dp'), axis=0)]
    unnamed x4, waiting for transfers between devices: 98.2 us -> 109 us
    unnamed x22 -> x23, local copies, waits for them, and re-layouts: 30.3 us -> 30.3 us
  transfers between devices with their start and end apart: 3 -> 3, of which waited for: 3 -> 3; matrix products, arithmetic and copies ran while one was open for 4% -> 5% of each run, Pallas kernels for 0% -> 0%
where the time goes in v1:
time: 324 us; the launch traced here: 323 us
  waiting for transfers between devices  206 us (64%)
  blocking collectives  35.9 us (11%)
  local copies, waits for them, and re-layouts  31.5 us (10%)
  matrix products  24.5 us (8%)
  between operations  13.8 us (4%)
  other arithmetic  12 us (4%)
    unnamed x4, waiting for transfers between devices  109 us
    reduce_scatter x1, waiting for transfers between devices, per_device(): lax.psum_scatter(partial_value, 'mp', scatter_dimension=1, tiled=True)  60.8 us
    all_gather x1, waiting for transfers between devices, per_device(): grad_attn = lax.all_gather(grad_half, 'mp', axis=1, tiled=True)  35.4 us
    unnamed x23, local copies, waits for them, and re-layouts  30.3 us
    all_gather x1, blocking collectives, per_device(): gain_total = jnp.sum(lax.all_gather(gain_part, 'dp'), axis=0)  21.6 us
    dot_general x1, matrix products, per_device(): lax.dot_general(context, grad_attn, (((0,), (0,)), ((), ())), preferred_e...  8.95 us
    dot_general x1, matrix products, per_device(): lax.dot_general(grad_attn, out_weight, (((1,), (1,)), ((), ())), preferre...  7.86 us
    dot_general x1, matrix products, per_device(): jnp.dot(context, out_weight, preferred_element_type=jnp.float32)  7.67 us
  transfers between devices with their start and end apart: 3, of which 3 were waited for; matrix products, arithmetic and copies ran while one was open for 5% of the time, Pallas kernels for 0%

profile of v1, /device:TPU:0, one launch (start us, length us, event | category | flops | bytes accessed | tf_op | source)
XLA Modules:
  0.0 323.4 jit_solution(14765775029541897819)
XLA Ops:
  7.2 1.0 copy-done
  8.3 7.7 %fusion.10 = f32[320,3584]{1,0:T(8,128)} fusion(bf16[320,1024]{1,0:T(8,128)(2,1)S(1)} %copy-done, bf16[1024,3584]{1,0:T(8,128)(2,1)} %param.7), kind=kOutput, calls=%fused_computation.20 | convolution fusion | flops 2348810240 | bytes 12582912 | tf_op jit(solution)/shard_map/dot_general | solution.py:24
  16.0 0.6 copy-done.5
  16.7 60.8 %reduce-scatter.5.cloned.1.call-done = f32[320,1792]{1,0:T(8,128)} async-done(((f32[320,3584]{1,0:T(8,128)}), f32[320,1792]{1,0:T(8,128)}) %reduce-scatter.5.cloned.1.call-update) | async-done | bytes 2293776 | tf_op jit(solution)/shard_map/reduce_scatter | solution.py:27
  77.5 2.0 multiply_reduce_fusion
  79.5 4.9 %psum.14 = f32[320,1]{0,1:T(1,128)S(1)} all-reduce(f32[320,1]{0,1:T(1,128)S(1)} %broadcast_in_dim.16), channel_id=1, replica_groups=mesh['dp'=16,'mp'=2] {'mp'}, use_global_device_ids=true, to_apply=%region_2.0 | all-reduce | flops 320 | bytes 2560 | tf_op jit(solution)/shard_map/psum | solution.py:31
  84.5 2.1 fusion.5
  86.6 4.9 %psum.15 = f32[320,1]{0,1:T(1,128)S(1)} all-reduce(f32[320,1]{0,1:T(1,128)S(1)} %broadcast_in_dim.17), channel_id=1, replica_groups=mesh['dp'=16,'mp'=2] {'mp'}, use_global_device_ids=true, to_apply=%region_4.0 | all-reduce | flops 320 | bytes 2560 | tf_op jit(solution)/shard_map/psum | solution.py:36
  91.5 2.8 fusion.4
  94.4 35.4 %all-gather.5.cloned.1.call-done = bf16[320,3584]{1,0:T(8,128)(2,1)} async-done(((bf16[320,1792]{1,0:T(8,128)(2,1)}), bf16[320,3584]{1,0:T(8,128)(2,1)}) %all-gather.5.cloned.1.call-update) | async-done | bytes 2293776 | tf_op jit(solution)/shard_map/all_gather | solution.py:38
  129.8 8.9 %convolution_bitcast_fusion = f32[1024,3584]{0,1:T(8,128)} fusion(bf16[320,3584]{1,0:T(8,128)(2,1)} %all-gather.5.cloned.1.call-done, bf16[320,1024]{1,0:T(8,128)(2,1)S(1)} %copy-done), kind=kOutput, calls=%fused_computation | convolution fusion | flops 2348810240 | bytes 17629184 | tf_op jit(solution)/shard_map/dot_general | solution.py:47
  138.8 14.3 %copy.29 = f32[1024,3584]{1,0:T(8,128)} copy(f32[1024,3584]{0,1:T(8,128)} %convolution_bitcast_fusion) | data formatting | bytes 29360128
  153.1 1.1 constant_dynamic-slice_fusion
  154.6 1.7 copy.24
  156.4 3.0 copy.25
  159.3 21.6 %all-gather.1 = f32[16,1,1792]{2,1,0:T(1,128)S(1)} all-gather(f32[1,1,1792]{2,1,0:T(1,128)S(1)} %reshape.16), channel_id=2, replica_groups=mesh['dp'=16,'mp'=2] {'dp'}, dimensions={0}, use_global_device_ids=true | all-gather | bytes 121856 | tf_op jit(solution)/shard_map/all_gather | solution.py:40
  181.0 4.4 %all-gather.2 = f32[2,1,1792]{2,1,0:T(1,128)S(1)} all-gather(f32[1,1,1792]{2,1,0:T(1,128)S(1)} %reshape.18), channel_id=1, replica_groups=mesh['dp'=16,'mp'=2] {'mp'}, dimensions={0}, use_global_device_ids=true | all-gather | bytes 21504 | tf_op jit(solution)/shard_map/all_gather | solution.py:41
  186.1 7.9 %convolution_convert_fusion = bf16[320,1024]{1,0:T(8,128)(2,1)} fusion(bf16[320,3584]{1,0:T(8,128)(2,1)} %all-gather.5.cloned.1.call-done, bf16[1024,3584]{1,0:T(8,128)(2,1)} %param.7), kind=kOutput, calls=%fused_computation.16 | convolution fusion | flops 2349137920 | bytes 10289152 | tf_op jit(solution)/shard_map/dot_general | solution.py:54
  194.0 109.4 %reduce-scatter.7.cloned.1.call-done = f32[64,3584]{1,0:T(8,128)} async-done(((f32[1024,3584]{1,0:T(8,128)}), f32[64,3584]{1,0:T(8,128)}) %reduce-scatter.7.cloned.1.call-update) | async-done | bytes 917520
  303.4 3.0 copy.30
  306.4 4.9 %fusion.8 = (bf16[1,64,3584]{1,2,0:T(8,128)(2,1)}, f32[1,64,3584]{1,2,0:T(8,128)}, f32[1,64,3584]{1,2,0:T(8,128)}) fusion(bf16[64,3584]{0,1:T(8,128)(2,1)S(1)} %copy.31, f32[64,3584]{0,1:T(8,128)} %copy.30, f32[1,64,3584]{1,2,0:T(8,128)S(1)} %copy.24, f32[1,64,3584]{1,2,0:T(8,128)} %copy.25), kind=kLoop, calls=%fused_computation.14 | loop fusion | flops 2981888 | bytes 5505024 | tf_op jit(solution)/shard_map/convert_element_type | solution.py:16
  311.3 3.1 copy.27
  314.4 1.4 copy.28
  315.8 1.1 copy.26
  (27 shorter events, 1.5 us)
Async XLA Ops:
  7.2 1.1 copy-start
  7.2 70.3 %reduce-scatter.5.cloned.1.call-start = ((), (), s32[]{:S(2)}) async-start(), calls=%async_computation.2 | async-start | bytes 6881280 | tf_op jit(solution)/shard_map/reduce_scatter | solution.py:27
  15.9 0.7 copy-start.5
  16.0 113.9 %all-gather.5.cloned.1.call-start = ((), (), s32[]{:S(2)}) async-start(), calls=%async_computation.3 | async-start | bytes 3440640 | tf_op jit(solution)/shard_map/all_gather | solution.py:38
  77.5 7.0 %copy-start.2 = (f32[320,1792]{1,0:T(8,128)S(1)}, f32[320,1792]{1,0:T(8,128)}, u32[]{:S(2)}) copy-start(f32[320,1792]{1,0:T(8,128)} %reduce-scatter.5.cloned.1.call-done) | copy-start | bytes 6881284
  94.4 209.0 %reduce-scatter.7.cloned.1.call-start = ((), (), s32[]{:S(2)}) async-start(), calls=%async_computation.4 | async-start | bytes 15597568
  311.3 3.1 copy-start.3
  311.3 4.5 %copy-start.4 = (bf16[1,64,3584]{1,2,0:T(8,128)(2,1)S(1)}, bf16[1,64,3584]{1,2,0:T(8,128)(2,1)}, u32[]{:S(2)}) copy-start(bf16[1,64,3584]{1,2,0:T(8,128)(2,1)} %get-tuple-element.22) | copy-start | bytes 1376260
  311.3 5.6 %copy-start.1 = (bf16[320,1024]{1,0:T(8,128)(2,1)S(1)}, bf16[320,1024]{1,0:T(8,128)(2,1)}, u32[]{:S(2)}) copy-start(bf16[320,1024]{1,0:T(8,128)(2,1)} %param.6) | copy-start | bytes 1966084
Sparse Core Ops, SparseCore 0:
  16.1 61.3 reduce-scatter.4
  94.5 35.3 all-gather.4
  153.3 150.0 reduce-scatter.6
